TPU v7x, 256 devices: a whole 4x4x8 slice. The times are simulated.
256 devices in a mesh: block: 4 (over y), tok: 64 (over z, x, core).
Axes of the slice: x: 4, y: 4, z: 8, core: 2. Of those that a mesh axis runs over, the one named last changes fastest.
Arguments:
- queries: float32 [32768, 256], P(('block', 'tok')), may hold values from -6 to 6
- keys: float32 [32768, 256], P(('block', 'tok')), may hold values from -6 to 6
- values: float32 [32768, 256], P(('block', 'tok')), may hold values from -6 to 6
- rates: float32 [32768], P(('block', 'tok')), may hold values from 0.0001 to 0.001
- states: float32 [4, 3, 256, 256], P('block', None, 'tok'), may hold values from -0.375 to 0.375
- out_cot: float32 [32768, 256], P(('block', 'tok')), may hold values from -6 to 6
- final_cot: float32 [3, 256, 256], P(None, 'tok'), may hold values from -6 to 6
Outputs:
- d_queries: float32 [32768, 256], P(('block', 'tok'))
- d_keys: float32 [32768, 256], P(('block', 'tok'))
- d_values: float32 [32768, 256], P(('block', 'tok'))
- d_rates: float32 [32768], P(('block', 'tok'))
- d_states: float32 [4, 3, 256, 256], P('block', None, 'tok')
All inputs are finite; a program needn't handle non-finite values.
Results may differ from a plain program's by a relative error of at most 0.00029.
Values sent between devices are 32-bit elements; how exact they have to be, the bound alone decides.
A program may use at most 64 MiB of HBM per device.

v0:
```python
import jax
import jax.numpy as jnp
from jax import lax
from jax.sharding import PartitionSpec as P

EPS = 1e-06
HIGH = lax.Precision.HIGHEST


def copy_for_each(array, axis):
    devices = lax.axis_size(axis)
    return lax.all_to_all(
        jnp.broadcast_to(array[None], (devices, *array.shape)), axis, 0, 0, tiled=True
    )


def laid_out(tiles, dim):
    tiles = jnp.moveaxis(tiles, 0, dim)
    shape = tiles.shape
    return tiles.reshape(*shape[:dim], shape[dim] * shape[dim + 1], *shape[dim + 2 :])


def gather_directly(array, axis, dim):
    tiles = copy_for_each(array, axis)
    return laid_out(tiles, dim)


def split_up(array, dim, devices):
    before, after = (array.shape[:dim], array.shape[dim + 1 :])
    return jnp.moveaxis(array.reshape(*before, devices, -1, *after), dim, 0)


def sent_and_summed(array, axis, dim):
    tiles = split_up(array, dim, lax.axis_size(axis))
    arrived = lax.all_to_all(tiles, axis, split_axis=0, concat_axis=0, tiled=True)
    return arrived.sum(axis=0)


def from_behind(array, axis, by):
    devices = lax.axis_size(axis)
    pairs = [(i, i + by) for i in range(devices) if 0 <= i + by < devices]
    return lax.ppermute(array, axis, pairs)


def apply_fast(weights, inputs):
    first = jnp.dot(inputs, weights[0], precision=HIGH, preferred_element_type=jnp.float32)
    gate = jnp.dot(inputs, weights[1], precision=HIGH, preferred_element_type=jnp.float32)
    mixed = jax.nn.silu(first) * gate
    return jnp.dot(mixed, weights[2], precision=HIGH, preferred_element_type=jnp.float32)


def update_grad(weights, keys, values, rates):

    def loss(current):
        return -jnp.sum(rates[:, None] * apply_fast(current, keys) * values)

    return jax.grad(loss)(weights)


def norm_adjoint(incoming, shifted, own, row_norm, new_norm):
    inner = jnp.sum(incoming * shifted, axis=-1, keepdims=True)
    d_shifted = (
        row_norm / new_norm * incoming
        - row_norm * inner / (new_norm * new_norm * new_norm) * shifted
    )
    direct = d_shifted + inner / new_norm * own / row_norm
    return (d_shifted, direct)


def per_device(queries, keys, values, rates, states, out_cot, final_cot):
    groups = lax.axis_size("block")
    position = lax.axis_index("block")
    own_rows = states[0]
    gathered = gather_directly(own_rows, "tok", 1)
    _, apply_back = jax.vjp(apply_fast, gathered, queries)
    apply_state, d_queries = apply_back(out_cot)
    grad_part, second_back = jax.vjp(update_grad, gathered, keys, values, rates)
    grad_rows = sent_and_summed(grad_part, "tok", 1)
    shifted = own_rows - grad_rows
    row_norm = jnp.sqrt(jnp.sum(own_rows * own_rows, axis=-1, keepdims=True) + EPS)
    new_norm = jnp.sqrt(jnp.sum(shifted * shifted, axis=-1, keepdims=True) + EPS)
    zero_back = (
        jnp.zeros_like(gathered),
        jnp.zeros_like(keys),
        jnp.zeros_like(values),
        jnp.zeros_like(rates),
    )
    incoming = final_cot
    d_keys = jnp.zeros_like(keys)
    d_values = jnp.zeros_like(values)
    d_rates = jnp.zeros_like(rates)
    d_rows = jnp.zeros_like(own_rows)
    for section in range(groups):
        active = position == groups - 1 - section
        d_shifted, direct = norm_adjoint(incoming, shifted, own_rows, row_norm, new_norm)
        d_grad = gather_directly(-d_shifted, "tok", 1)
        second_state, second_keys, second_values, second_rates = lax.cond(
            active, lambda cot: second_back(cot), lambda cot: zero_back, d_grad
        )
        summed = sent_and_summed(second_state + apply_state, "tok", 1)
        rows_now = summed + direct
        d_keys = jnp.where(active, second_keys, d_keys)
        d_values = jnp.where(active, second_values, d_values)
        d_rates = jnp.where(active, second_rates, d_rates)
        d_rows = jnp.where(active, rows_now, d_rows)
        if section + 1 < groups:
            incoming = from_behind(rows_now, "block", -1)
    return (d_queries, d_keys, d_values, d_rates, d_rows[None])


def solution(mesh):
    return jax.shard_map(
        per_device,
        mesh=mesh,
        in_specs=(
            P(("block", "tok"), None),
            P(("block", "tok"), None),
            P(("block", "tok"), None),
            P(("block", "tok")),
            P("block", None, "tok", None),
            P(("block", "tok"), None),
            P(None, "tok", None),
        ),
        out_specs=(
            P(("block", "tok"), None),
            P(("block", "tok"), None),
            P(("block", "tok"), None),
            P(("block", "tok")),
            P("block", None, "tok", None),
        ),
        check_vma=False,
    )
```

profile of v0, /device:TPU:1, one launch (start us, length us, event | category | flops | bytes accessed | tf_op | source)
XLA Modules:
  0.0 444.0 jit_solution(15689715033276362109)
XLA Ops:
  2.4 13.1 %all-to-all-start = ((f32[64,3,4,256]{3,2,1,0:T(4,128)}), f32[64,3,4,256]{3,2,1,0:T(4,128)S(1)}, u32[]{:S(2)}, u32[]{:S(2)}) async-start(f32[64,3,4,256]{3,2,1,0:T(4,128)} %broadcast_in_dim.143), calls=%async_computation | async-start | bytes 1572864 | tf_op jit(solution)/shard_map/all_to_all | solution.py:12
  15.6 22.9 %all-to-all-done = f32[64,3,4,256]{3,2,1,0:T(4,128)S(1)} async-done(((f32[64,3,4,256]{3,2,1,0:T(4,128)}), f32[64,3,4,256]{3,2,1,0:T(4,128)S(1)}, u32[]{:S(2)}, u32[]{:S(2)}) %all-to-all-start) | async-done | bytes 786464 | tf_op jit(solution)/shard_map/all_to_all | solution.py:12
  45.3 28.8 %all_to_all.50 = f32[64,3,4,256]{3,2,1,0:T(4,128)} all-to-all(f32[64,3,4,256]{3,2,1,0:T(4,128)S(1)} %bitcast.220), channel_id=1, replica_groups=mesh['block'=4,'tok'=64] {'tok'}, dimensions={0} | all-to-all | bytes 1572864 | tf_op jit(solution)/shard_map/all_to_all | solution.py:35
  78.4 6.1 %all-to-all-start.2 = ((f32[64,3,4,256]{3,2,1,0:T(4,128)}), f32[64,3,4,256]{3,2,1,0:T(4,128)}, u32[]{:S(2)}, u32[]{:S(2)}) async-start(f32[64,3,4,256]{3,2,1,0:T(4,128)} %broadcast_in_dim.147), calls=%async_computation.2 | async-start | bytes 1572864 | tf_op jit(solution)/shard_map/all_to_all | solution.py:12
  87.4 20.0 %all-to-all-done.2 = f32[64,3,4,256]{3,2,1,0:T(4,128)} async-done(((f32[64,3,4,256]{3,2,1,0:T(4,128)}), f32[64,3,4,256]{3,2,1,0:T(4,128)}, u32[]{:S(2)}, u32[]{:S(2)}) %all-to-all-start.2) | async-done | bytes 786464 | tf_op jit(solution)/shard_map/all_to_all | solution.py:12
  107.4 2.9 conditional.4
  112.5 2.2 reshape.179
  116.0 28.8 %all_to_all.51 = f32[64,3,4,256]{3,2,1,0:T(4,128)} all-to-all(f32[64,3,4,256]{3,2,1,0:T(4,128)S(1)} %bitcast.221), channel_id=1, replica_groups=mesh['block'=4,'tok'=64] {'tok'}, dimensions={0} | all-to-all | bytes 1572864 | tf_op jit(solution)/shard_map/all_to_all | solution.py:35
  149.5 3.1 collective-permute-done
  155.0 7.2 %all-to-all-start.4 = ((f32[64,3,4,256]{3,2,1,0:T(4,128)}), f32[64,3,4,256]{3,2,1,0:T(4,128)}, u32[]{:S(2)}, u32[]{:S(2)}) async-start(f32[64,3,4,256]{3,2,1,0:T(4,128)} %broadcast_in_dim.154), calls=%async_computation.4 | async-start | bytes 1572864 | tf_op jit(solution)/shard_map/all_to_all | solution.py:12
  162.3 22.9 %all-to-all-done.4 = f32[64,3,4,256]{3,2,1,0:T(4,128)} async-done(((f32[64,3,4,256]{3,2,1,0:T(4,128)}), f32[64,3,4,256]{3,2,1,0:T(4,128)}, u32[]{:S(2)}, u32[]{:S(2)}) %all-to-all-start.4) | async-done | bytes 786464 | tf_op jit(solution)/shard_map/all_to_all | solution.py:12
  185.2 2.9 conditional.5
  193.7 29.0 %all_to_all.52 = f32[64,3,4,256]{3,2,1,0:T(4,128)} all-to-all(f32[64,3,4,256]{3,2,1,0:T(4,128)S(1)} %bitcast.222), channel_id=1, replica_groups=mesh['block'=4,'tok'=64] {'tok'}, dimensions={0} | all-to-all | bytes 1572864 | tf_op jit(solution)/shard_map/all_to_all | solution.py:35
  226.8 3.1 collective-permute-done.1
  232.3 7.2 %all-to-all-start.6 = ((f32[64,3,4,256]{3,2,1,0:T(4,128)}), f32[64,3,4,256]{3,2,1,0:T(4,128)}, u32[]{:S(2)}, u32[]{:S(2)}) async-start(f32[64,3,4,256]{3,2,1,0:T(4,128)} %broadcast_in_dim.155), calls=%async_computation.6 | async-start | bytes 1572864 | tf_op jit(solution)/shard_map/all_to_all | solution.py:12
  239.5 22.9 %all-to-all-done.6 = f32[64,3,4,256]{3,2,1,0:T(4,128)} async-done(((f32[64,3,4,256]{3,2,1,0:T(4,128)}), f32[64,3,4,256]{3,2,1,0:T(4,128)}, u32[]{:S(2)}, u32[]{:S(2)}) %all-to-all-start.6) | async-done | bytes 786464 | tf_op jit(solution)/shard_map/all_to_all | solution.py:12
  262.4 2.8 conditional.6
  270.9 28.8 %all_to_all.53 = f32[64,3,4,256]{3,2,1,0:T(4,128)} all-to-all(f32[64,3,4,256]{3,2,1,0:T(4,128)S(1)} %bitcast.223), channel_id=1, replica_groups=mesh['block'=4,'tok'=64] {'tok'}, dimensions={0} | all-to-all | bytes 1572864 | tf_op jit(solution)/shard_map/all_to_all | solution.py:35
  303.7 54.1 %collective-permute-done.2 = f32[3,4,256]{2,1,0:T(4,128)S(1)} collective-permute-done((f32[3,4,256]{2,1,0:T(4,128)S(1)}, f32[3,4,256]{2,1,0:T(4,128)S(1)}, u32[]{:S(2)}, u32[]{:S(2)}) %collective-permute-start.2) | collective-permute-done | bytes 12320 | tf_op jit(solution)/shard_map/ppermute | solution.py:42
  360.2 6.9 %all-to-all-start.8 = ((f32[64,3,4,256]{3,2,1,0:T(4,128)}), f32[64,3,4,256]{3,2,1,0:T(4,128)}, u32[]{:S(2)}, u32[]{:S(2)}) async-start(f32[64,3,4,256]{3,2,1,0:T(4,128)} %broadcast_in_dim.156), calls=%async_computation.8 | async-start | bytes 1572864 | tf_op jit(solution)/shard_map/all_to_all | solution.py:12
  367.1 22.9 %all-to-all-done.8 = f32[64,3,4,256]{3,2,1,0:T(4,128)} async-done(((f32[64,3,4,256]{3,2,1,0:T(4,128)}), f32[64,3,4,256]{3,2,1,0:T(4,128)}, u32[]{:S(2)}, u32[]{:S(2)}) %all-to-all-start.8) | async-done | bytes 786464 | tf_op jit(solution)/shard_map/all_to_all | solution.py:12
  390.1 19.8 %conditional.7 = (f32[3,256,256]{2,1,0:T(8,128)S(1)}, f32[128,256]{1,0:T(8,128)}, f32[128,256]{1,0:T(8,128)}, f32[128]{0:T(128)}) conditional(s32[]{:T(128)} %convert_element_type.12, () %tuple.51, (f32[3,64,4,256]{3,2,0,1:T(4,128)}, f32[128,256]{1,0:T(8,128)S(1)}, f32[128,256]{1,0:T(8,128)}, f32[128,256]{1,0:T(8,128)}, f32[128,256]{1,0:T(8,128)S(1)}, ...), branch_computations={%region_19.20_spmd, %region_20.22_spmd} | conditional | flops 1209499520 | bytes 19795200 | solution.py:97
  413.3 5.9 %all-to-all-start.9 = ((f32[64,3,4,256]{3,2,1,0:T(4,128)}), f32[64,3,4,256]{3,2,1,0:T(4,128)S(1)}, u32[]{:S(2)}, u32[]{:S(2)}) async-start(f32[64,3,4,256]{3,2,1,0:T(4,128)} %bitcast.214), calls=%async_computation.9 | async-start | bytes 1572864 | tf_op jit(solution)/shard_map/all_to_all | solution.py:35
  424.1 18.1 %all-to-all-done.9 = f32[64,3,4,256]{3,2,1,0:T(4,128)S(1)} async-done(((f32[64,3,4,256]{3,2,1,0:T(4,128)}), f32[64,3,4,256]{3,2,1,0:T(4,128)S(1)}, u32[]{:S(2)}, u32[]{:S(2)}) %all-to-all-start.9) | async-done | bytes 786464 | tf_op jit(solution)/shard_map/all_to_all | solution.py:35
  (185 shorter events, 87.5 us)
Async XLA Ops:
  0.6 83.9 %copy-start = (f32[128,256]{1,0:T(8,128)S(1)}, f32[128,256]{1,0:T(8,128)}, u32[]{:S(2)}) copy-start(f32[128,256]{1,0:T(8,128)} %param.15) | copy-start | bytes 393220
  2.4 13.1 %copy-start.63 = (f32[128]{0:T(128)S(1)}, f32[128]{0:T(128)}, u32[]{:S(2)}) copy-start(f32[128]{0:T(128)} %param.18) | copy-start | bytes 1540
  2.4 13.1 %copy-start.36 = (f32[128,256]{1,0:T(8,128)S(1)}, f32[128,256]{1,0:T(8,128)}, u32[]{:S(2)}) copy-start(f32[128,256]{1,0:T(8,128)} %param.17) | copy-start | bytes 393220
  2.4 36.1 %all-to-all-start = ((f32[64,3,4,256]{3,2,1,0:T(4,128)}), f32[64,3,4,256]{3,2,1,0:T(4,128)S(1)}, u32[]{:S(2)}, u32[]{:S(2)}) async-start(f32[64,3,4,256]{3,2,1,0:T(4,128)} %broadcast_in_dim.143), calls=%async_computation | async-start | bytes 1572864 | tf_op jit(solution)/shard_map/all_to_all | solution.py:12
  78.4 29.0 %all-to-all-start.2 = ((f32[64,3,4,256]{3,2,1,0:T(4,128)}), f32[64,3,4,256]{3,2,1,0:T(4,128)}, u32[]{:S(2)}, u32[]{:S(2)}) async-start(f32[64,3,4,256]{3,2,1,0:T(4,128)} %broadcast_in_dim.147), calls=%async_computation.2 | async-start | bytes 1572864 | tf_op jit(solution)/shard_map/all_to_all | solution.py:12
  148.2 4.6 %copy-start.52 = (f32[3,4,256]{2,1,0:T(4,128)}, f32[3,4,256]{2,1,0:T(4,128)S(1)}, u32[]{:S(2)}) copy-start(f32[3,4,256]{2,1,0:T(4,128)S(1)} %fusion.14) | copy-start | bytes 36868
  148.2 4.6 %copy-start.43 = (f32[3,4]{1,0:T(4,128)S(1)}, f32[3,4]{1,0:T(4,128)}, u32[]{:S(2)}) copy-start(f32[3,4]{1,0:T(4,128)} %copy-done.42) | copy-start | bytes 148
  148.2 4.4 collective-permute-start
  155.0 30.2 %all-to-all-start.4 = ((f32[64,3,4,256]{3,2,1,0:T(4,128)}), f32[64,3,4,256]{3,2,1,0:T(4,128)}, u32[]{:S(2)}, u32[]{:S(2)}) async-start(f32[64,3,4,256]{3,2,1,0:T(4,128)} %broadcast_in_dim.154), calls=%async_computation.4 | async-start | bytes 1572864 | tf_op jit(solution)/shard_map/all_to_all | solution.py:12
  225.4 4.6 %copy-start.54 = (f32[3,4,256]{2,1,0:T(4,128)}, f32[3,4,256]{2,1,0:T(4,128)S(1)}, u32[]{:S(2)}) copy-start(f32[3,4,256]{2,1,0:T(4,128)S(1)} %fusion.15) | copy-start | bytes 36868
  225.5 4.4 collective-permute-start.1
  232.3 30.2 %all-to-all-start.6 = ((f32[64,3,4,256]{3,2,1,0:T(4,128)}), f32[64,3,4,256]{3,2,1,0:T(4,128)}, u32[]{:S(2)}, u32[]{:S(2)}) async-start(f32[64,3,4,256]{3,2,1,0:T(4,128)} %broadcast_in_dim.155), calls=%async_computation.6 | async-start | bytes 1572864 | tf_op jit(solution)/shard_map/all_to_all | solution.py:12
  302.4 55.6 %copy-start.56 = (f32[3,4,256]{2,1,0:T(4,128)}, f32[3,4,256]{2,1,0:T(4,128)S(1)}, u32[]{:S(2)}) copy-start(f32[3,4,256]{2,1,0:T(4,128)S(1)} %fusion.16) | copy-start | bytes 36868
  302.4 55.5 %copy-start.45 = (f32[3,4]{1,0:T(4,128)S(1)}, f32[3,4]{1,0:T(4,128)}, u32[]{:S(2)}) copy-start(f32[3,4]{1,0:T(4,128)} %copy-done.42) | copy-start | bytes 148
  302.4 55.5 %copy-start.49 = (f32[3,4]{1,0:T(4,128)S(1)}, f32[3,4]{1,0:T(4,128)}, u32[]{:S(2)}) copy-start(f32[3,4]{1,0:T(4,128)} %copy-done.46) | copy-start | bytes 148
  302.4 55.4 %collective-permute-start.2 = (f32[3,4,256]{2,1,0:T(4,128)S(1)}, f32[3,4,256]{2,1,0:T(4,128)S(1)}, u32[]{:S(2)}, u32[]{:S(2)}) collective-permute-start(f32[3,4,256]{2,1,0:T(4,128)S(1)} %fusion.16), channel_id=1, source_target_pairs={{64,0},{128,64},{192,128},{65,1},{129,65},{193,129},{66,2},{130,66... | collective-permute-start | bytes 36872 | tf_op jit(solution)/shard_map/ppermute | solution.py:42
  360.2 29.9 %all-to-all-start.8 = ((f32[64,3,4,256]{3,2,1,0:T(4,128)}), f32[64,3,4,256]{3,2,1,0:T(4,128)}, u32[]{:S(2)}, u32[]{:S(2)}) async-start(f32[64,3,4,256]{3,2,1,0:T(4,128)} %broadcast_in_dim.156), calls=%async_computation.8 | async-start | bytes 1572864 | tf_op jit(solution)/shard_map/all_to_all | solution.py:12
  413.3 28.9 %all-to-all-start.9 = ((f32[64,3,4,256]{3,2,1,0:T(4,128)}), f32[64,3,4,256]{3,2,1,0:T(4,128)S(1)}, u32[]{:S(2)}, u32[]{:S(2)}) async-start(f32[64,3,4,256]{3,2,1,0:T(4,128)} %bitcast.214), calls=%async_computation.9 | async-start | bytes 1572864 | tf_op jit(solution)/shard_map/all_to_all | solution.py:35
  422.3 20.0 %copy-start.51 = (f32[3,4]{1,0:T(4,128)S(1)}, f32[3,4]{1,0:T(4,128)}, u32[]{:S(2)}) copy-start(f32[3,4]{1,0:T(4,128)} %get-tuple-element.424) | copy-start | bytes 148
  424.1 18.3 %copy-start.35 = (f32[1,3,4,256]{3,2,1,0:T(4,128)S(1)}, f32[1,3,4,256]{3,2,1,0:T(4,128)}, u32[]{:S(2)}) copy-start(f32[1,3,4,256]{3,2,1,0:T(4,128)} %param.19) | copy-start | bytes 36868
  424.1 18.3 %copy-start.39 = (f32[3,4,256]{2,1,0:T(4,128)S(1)}, f32[3,4,256]{2,1,0:T(4,128)}, u32[]{:S(2)}) copy-start(f32[3,4,256]{2,1,0:T(4,128)} %copy-done.38) | copy-start | bytes 36868
  424.1 18.3 %copy-start.53 = (f32[3,4,256]{2,1,0:T(4,128)S(1)}, f32[3,4,256]{2,1,0:T(4,128)}, u32[]{:S(2)}) copy-start(f32[3,4,256]{2,1,0:T(4,128)} %copy-done.52) | copy-start | bytes 36868
  424.1 18.3 %copy-start.55 = (f32[3,4,256]{2,1,0:T(4,128)S(1)}, f32[3,4,256]{2,1,0:T(4,128)}, u32[]{:S(2)}) copy-start(f32[3,4,256]{2,1,0:T(4,128)} %copy-done.54) | copy-start | bytes 36868
  424.1 18.3 %copy-start.57 = (f32[3,4,256]{2,1,0:T(4,128)S(1)}, f32[3,4,256]{2,1,0:T(4,128)}, u32[]{:S(2)}) copy-start(f32[3,4,256]{2,1,0:T(4,128)} %copy-done.56) | copy-start | bytes 36868
  (30 other events, 38.3 us)
where the time goes:
time: 452 us; the launch traced here: 444 us
  waiting for transfers between devices  190 us (42%)
  blocking collectives  115 us (25%)
  starting transfers between devices  50.4 us (11%)
  local copies, waits for them, and re-layouts  44.5 us (10%)
  other arithmetic  24.1 us (5%)
  matrix products  17.3 us (4%)
    all_to_all x4, blocking collectives, sent_and_summed(): lax.all_to_all(tiles, axis, split_axis=0, concat_axis=0, tiled=True)  115 us
    all_to_all x5, waiting for transfers between devices, copy_for_each(): lax.all_to_all(jnp.broadcast_to(array[None], (devices, *array.shape)), ax...  112 us
    ppermute x3, waiting for transfers between devices, from_behind(): return lax.ppermute(array, axis, pairs)  60.4 us
    all_to_all x5, starting transfers between devices, copy_for_each(): lax.all_to_all(jnp.broadcast_to(array[None], (devices, *array.shape)), ax...  40.6 us
    all_to_all x1, waiting for transfers between devices, sent_and_summed(): lax.all_to_all(tiles, axis, split_axis=0, concat_axis=0, tiled=True)  18.1 us
    reshape x10, local copies, waits for them, and re-layouts, split_up(): return jnp.moveaxis(array.reshape(*before, devices, -1, *after), dim, 0)  14.2 us
  transfers between devices with their start and end apart: 9, of which 9 were waited for; matrix products, arithmetic and copies ran while one was open for 2% of the time, Pallas kernels for 0%

commit v1 on v0

v1 whole, which is shorter than its diff:
```python
import functools

import jax
import jax.numpy as jnp
from jax import lax
from jax.experimental import pallas as pl
from jax.experimental.pallas import tpu as pltpu
from jax.sharding import PartitionSpec as P

EPS = 1e-06
F32 = jnp.float32
BF16 = jnp.bfloat16
D = 256
HALF = 128
NZ, NX = 8, 4
NN = (((1,), (0,)), ((), ()))
NT = (((1,), (1,)), ((), ()))
TN = (((0,), (0,)), ((), ()))
FAR_FIRST = (4, 3, 5, 2, 6, 1, 7)
NEAR_FIRST = (0, 1, 7, 2, 6, 3, 5, 4)


def split(a):
    hi = a.astype(BF16)
    return hi, (a - hi.astype(F32)).astype(BF16)


def dot1(a, b, dims):
    return lax.dot_general(a, b, dims, preferred_element_type=F32)


def dot3(a, b, dims):
    return dot1(a[0], b[0], dims) + (dot1(a[0], b[1], dims) + dot1(a[1], b[0], dims))


def exact_select(a, one_hot):
    hi = a.astype(BF16)
    rest = a - hi.astype(F32)
    mid = rest.astype(BF16)
    low = (rest - mid.astype(F32)).astype(BF16)
    return (dot1(hi, one_hot, NN) + dot1(mid, one_hot, NN)) + dot1(low, one_hot, NN)


def silu_parts(u):
    sig = 1.0 / (1.0 + jnp.exp(-u))
    return sig, u * sig, sig * (1.0 + u * (1.0 - sig))


def kernel(
    q_in, k_in, v_in, r_in, s_in, oc_in, fc_in,
    dq_out, dk_out, dv_out, dr_out, ds_out,
    k_sib, v_sib, q_sib, oc_sib, r_own, r_sib,
    own_w, own_z, rows_z, z_in, nat,
    g_w, g_d, p_g, p_z, rx_g, rx_z, rza_g, rzb_g, rza_z, rzb_z, sum_g, sum_z,
    w13, w2, d13, d2, ap13, ap2, t13, t2,
    kh, kl, kth, ktl, vh, vl,
    w13h, w13l, w2h, w2l, d13h, d13l, d2h, d2l,
    c_uu, c_ug, c_uq, c_gq, g_ug, g_q, a_ug, a_q,
    part_q, part_k, part_v, part_r, fin_q, fin_k, fin_v, fin_r,
    sib_s, sib_r,
    agw_s, agw_za, agw_zb, agw_x, agd_s, agd_za, agd_zb, agd_x,
    rsg_s, rsg_x, rsg_z, rsz_s, rsz_x, rsz_z,
    y_sem, fin_s, fin_r_sem,
):
    y = lax.axis_index("block")
    t = lax.axis_index("tok")
    core = lax.rem(t, 2)
    x = lax.rem(lax.div(t, 2), NX)
    z = lax.div(t, 2 * NX)

    def tok(zz, xx, cc):
        return (zz * NX + xx) * 2 + cc

    def ahead(a, by, n):
        return lax.rem(a + by, n)

    sibling = tok(z, x, 1 - core)

    def send(src, dst, s_sem, r_sem, to):
        pltpu.make_async_remote_copy(
            src_ref=src, dst_ref=dst, send_sem=s_sem, recv_sem=r_sem,
            device_id=(y, to), device_id_type=pl.DeviceIdType.MESH,
        ).start()

    def wait(ref, sem):
        pltpu.make_async_copy(ref, ref, sem).wait()

    barrier = pltpu.get_barrier_semaphore()

    def greet(block, to):
        pl.semaphore_signal(barrier, inc=1, device_id=(block, to), device_id_type=pl.DeviceIdType.MESH)

    for d in FAR_FIRST:
        greet(y, tok(ahead(z, d, NZ), x, core))
        greet(y, tok(ahead(z, d, NZ), x, 1 - core))
    for dx in (2, 1, 3):
        greet(y, tok(z, ahead(x, dx, NX), core))
    greet(y, sibling)
    greet(ahead(y, 1, 4), t)
    greet(ahead(y, 3, 4), t)

    row_i = lax.broadcasted_iota(jnp.int32, (D, D), 0)
    col_i = lax.broadcasted_iota(jnp.int32, (D, D), 1)

    def hidden_of(p):
        return 8 * ((p & 127) >> 2) + 4 * (p >> 7) + (p & 3)

    top = lax.broadcasted_iota(jnp.int32, (8, HALF), 0) < 4

    def half_swap(a):
        return pltpu.roll(a, 4, 0)

    def pick(first, second):
        return jnp.where(core == 0, first, second)

    def to_own(ref3, out):
        nat[0:4, :] = ref3[0]
        nat[4:8, :] = ref3[1]
        nat[8:12, :] = ref3[2]
        one_hot = (row_i == hidden_of(col_i)).astype(F32).astype(BF16)
        a = exact_select(nat[0:8, :], one_hot)
        out[0:8, :] = pick(a[:, :HALF], a[:, HALF:])
        out[16:24, :] = pick(a[:, HALF:], a[:, :HALF])
        b = nat[8:16, :]
        out[8:16, :] = jnp.where(top, b[:, :HALF], half_swap(b[:, HALF:]))

    nat[...] = jnp.zeros_like(nat)
    to_own(s_in.at[0], own_w)
    r_own[...] = jnp.broadcast_to(r_in[...], (8, HALF))

    pl.semaphore_wait(barrier, 20)

    pairs = ((k_in, k_sib), (v_in, v_sib), (q_in, q_sib), (oc_in, oc_sib), (r_own, r_sib))

    def share(n):
        send(pairs[n][0], pairs[n][1], sib_s.at[n], sib_r.at[n], sibling)

    def gather_start(own, g, sems, za, zb):
        g[x, z, 0:16, :] = own[0:16, :]
        for d in FAR_FIRST:
            zp = ahead(z, d, NZ)
            send(own.at[0:16], g.at[x, z, 0:16], sems.at[0], za.at[d], tok(zp, x, core))
            send(own.at[16:24], g.at[x, z, 16:24], sems.at[1], zb.at[d], tok(zp, x, 1 - core))
        send(own.at[16:24], g.at[x, z, 16:24], sems.at[1], zb.at[0], sibling)

    def gather_finish(g, sems, za, zb, xs):
        for d in NEAR_FIRST:
            zs = ahead(z, NZ - d, NZ)
            if d:
                wait(g.at[x, zs, 0:16], za.at[d])
            wait(g.at[x, zs, 16:24], zb.at[d])
            for dx in (2, 1, 3):
                send(g.at[x, zs], g.at[x, zs], sems.at[2], xs, tok(z, ahead(x, dx, NX), core))
        wait(g.at[0:3], xs)

    def gather_sent(g, sems):
        wait(rza_g, sems.at[0])
        wait(rzb_g, sems.at[1])
        wait(g.at[0:3], sems.at[2])

    def assemble(g, w13_ref, w2_ref):
        def step(zz, carry):
            for xx in range(NX):
                same, other = g[xx, zz, 0:8, :], g[xx, zz, 16:24, :]
                a0, a1 = pick(same, other), pick(other, same)
                rows = pl.ds(pl.multiple_of(zz * 32 + 8 * xx, 8), 8)
                w13_ref[rows, :HALF] = jnp.where(top, a0, half_swap(a1))
                w13_ref[rows, HALF:] = jnp.where(top, half_swap(a0), a1)
            for pr in range(2):
                b0, b1 = g[2 * pr, zz, 8:16, :], g[2 * pr + 1, zz, 8:16, :]
                rows = pl.ds(pl.multiple_of(zz * 16 + 8 * pr, 8), 8)
                w2_ref[rows, :HALF] = jnp.where(top, b0, half_swap(b1))
                w2_ref[rows, HALF:] = jnp.where(top, half_swap(b0), b1)
            return carry

        lax.fori_loop(0, NZ, step, 0)

    def pieces(w13_ref, w2_ref, p):
        def step(zz, carry):
            for xx in range(NX):
                rows = pl.ds(pl.multiple_of(zz * 32 + 8 * xx, 8), 8)
                first, gate = w13_ref[rows, :HALF], w13_ref[rows, HALF:]
                a0 = jnp.where(top, first, half_swap(gate))
                a1 = jnp.where(top, half_swap(first), gate)
                p[xx, zz, 0:8, :] = pick(a0, a1)
                p[xx, zz, 16:24, :] = pick(a1, a0)
            for pr in range(2):
                rows = pl.ds(pl.multiple_of(zz * 16 + 8 * pr, 8), 8)
                c0, c1 = w2_ref[rows, :HALF], w2_ref[rows, HALF:]
                p[2 * pr, zz, 8:16, :] = jnp.where(top, c0, half_swap(c1))
                p[2 * pr + 1, zz, 8:16, :] = jnp.where(top, half_swap(c0), c1)
            return carry

        lax.fori_loop(0, NZ, step, 0)

    def sum_start(p, rx, sems, xs):
        for d in FAR_FIRST + (0,):
            zp = ahead(z, d, NZ)
            for dx in (2, 1, 3):
                xp = ahead(x, dx, NX)
                send(p.at[xp, zp], rx.at[dx - 1, d], sems.at[0], xs.at[d], tok(z, xp, core))

    def sum_middle(p, rx, total, sems, xs, rza, rzb, zs):
        for d in FAR_FIRST + (0,):
            zp = ahead(z, d, NZ)
            wait(rx.at[:, d], xs.at[d])
            total[d] = (p[x, zp] + rx[0, d]) + (rx[1, d] + rx[2, d])
            if d:
                send(total.at[d, 0:16], rza.at[d - 1], sems.at[1], zs.at[0], tok(zp, x, core))
            send(total.at[d, 16:24], rzb.at[d], sems.at[2], zs.at[1], tok(zp, x, 1 - core))

    def sum_finish(total, rza, rzb, zs):
        wait(rza, zs.at[0])
        wait(rzb, zs.at[1])
        return jnp.concatenate(
            [total[0, 0:16, :] + jnp.sum(rza[...], axis=0), jnp.sum(rzb[...], axis=0)], axis=0
        )

    def sum_sent(p, rza, rzb, sems):
        wait(p.at[0:3], sems.at[0])
        wait(rza, sems.at[1])
        wait(rzb, sems.at[2])

    gather_start(own_w, g_w, agw_s, agw_za, agw_zb)
    for n in range(5):
        share(n)

    wait(k_sib, sib_r.at[0])
    keys = jnp.concatenate([k_in[...], k_sib[...]], axis=0)
    kh[...], kl[...] = split(keys)
    kth[...], ktl[...] = split(keys.T)
    wait(v_sib, sib_r.at[1])
    vh[...], vl[...] = split(jnp.concatenate([v_in[...], v_sib[...]], axis=0))
    wait(r_sib, sib_r.at[4])

    def columns_of(rows8):
        return jnp.broadcast_to(rows8[0:1, :], (HALF, HALF)).T

    rate = jnp.concatenate([columns_of(r_own[...]), columns_of(r_sib[...])], axis=0)

    gather_finish(g_w, agw_s, agw_za, agw_zb, agw_x)
    assemble(g_w, w13, w2)
    w13h[...], w13l[...] = split(w13[...])
    w2h[...], w2l[...] = split(w2[...])

    k_pair, kt_pair, v_pair = (kh[...], kl[...]), (kth[...], ktl[...]), (vh[...], vl[...])
    ug = dot3(k_pair, (w13h[...], w13l[...]), NN)
    inner_v = dot3(v_pair, (w2h[...], w2l[...]), NT)
    u, gate = ug[:, :HALF], ug[:, HALF:]
    sig, s0, s1 = silu_parts(u)
    uq = -rate * s1 * gate
    gq = -rate * s0
    grad_u, grad_g, grad_q = uq * inner_v, gq * inner_v, gq * gate
    grad_ug = jnp.concatenate([grad_u, grad_g], axis=1)
    t13[...] = dot3(kt_pair, split(grad_ug), NN)
    t2[...] = dot3(split(grad_q), v_pair, TN)
    pieces(t13, t2, p_g)
    sum_start(p_g, rx_g, rsg_s, rsg_x)
    c_uq[...] = uq
    c_gq[...] = gq
    c_ug[...] = -rate * s1 * inner_v
    c_uu[...] = -rate * (sig * (1.0 - sig) * (2.0 + u * (1.0 - 2.0 * sig))) * gate * inner_v
    g_ug[...] = grad_ug
    g_q[...] = grad_q
    sum_middle(p_g, rx_g, sum_g, rsg_s, rsg_x, rza_g, rzb_g, rsg_z)

    wait(q_sib, sib_r.at[2])
    wait(oc_sib, sib_r.at[3])
    queries = jnp.concatenate([q_in[...], q_sib[...]], axis=0)
    cot_pair = split(jnp.concatenate([oc_in[...], oc_sib[...]], axis=0))
    w13_pair, w2_pair = (w13h[...], w13l[...]), (w2h[...], w2l[...])
    q_ug = dot3(split(queries), w13_pair, NN)
    d_mixed = dot3(cot_pair, w2_pair, NT)
    q_u, q_gate = q_ug[:, :HALF], q_ug[:, HALF:]
    _, qs0, qs1 = silu_parts(q_u)
    back = split(jnp.concatenate([d_mixed * q_gate * qs1, d_mixed * qs0], axis=1))
    ap13[...] = dot3(split(queries.T), back, NN)
    ap2[...] = dot3(split(qs0 * q_gate), cot_pair, TN)
    part_q[...] = dot3(back, w13_pair, NT)
    send(part_q.at[HALF:], fin_q, fin_s.at[0], fin_r_sem.at[0], sibling)

    def row_sums(a, b):
        prod = a * b
        first = jnp.sum(prod[0:8] + prod[16:24], axis=-1, keepdims=True)
        second = jnp.sum(prod[8:16] + half_swap(prod[8:16]), axis=-1, keepdims=True)
        return jnp.concatenate([first, second, first], axis=0)

    own = own_w[...]
    row_norm = jnp.sqrt(row_sums(own, own) + EPS)
    shifted = own - sum_finish(sum_g, rza_g, rzb_g, rsg_z)
    new_norm = jnp.sqrt(row_sums(shifted, shifted) + EPS)

    @pl.when(y == 3)
    def _():
        to_own(fc_in, z_in)

    @pl.when(y < 3)
    def _():
        wait(z_in, y_sem.at[1])

    incoming = z_in[...]
    inner = row_sums(incoming, shifted)
    d_shifted = row_norm / new_norm * incoming - row_norm * inner / (new_norm * new_norm * new_norm) * shifted
    direct = d_shifted + inner / new_norm * own / row_norm
    own_z[...] = -d_shifted
    gather_start(own_z, g_d, agd_s, agd_za, agd_zb)
    gather_finish(g_d, agd_s, agd_za, agd_zb, agd_x)
    assemble(g_d, d13, d2)
    d13h[...], d13l[...] = split(d13[...])
    d2h[...], d2l[...] = split(d2[...])

    d13_pair, d2_pair = (d13h[...], d13l[...]), (d2h[...], d2l[...])
    ug_dot = dot3(k_pair, d13_pair, NN)
    q_dot = dot3(v_pair, d2_pair, NT)
    u_dot, g_dot = ug_dot[:, :HALF], ug_dot[:, HALF:]
    au = u_dot * c_uu[...] + g_dot * c_ug[...] + q_dot * c_uq[...]
    ag = u_dot * c_ug[...] + q_dot * c_gq[...]
    aq = u_dot * c_uq[...] + g_dot * c_gq[...]
    aug_pair = split(jnp.concatenate([au, ag], axis=1))
    aq_pair = split(aq)
    t13[...] = dot3(kt_pair, aug_pair, NN) + ap13[...]
    t2[...] = dot3(aq_pair, v_pair, TN) + ap2[...]
    pieces(t13, t2, p_z)
    sum_start(p_z, rx_z, rsz_s, rsz_x)
    sum_middle(p_z, rx_z, sum_z, rsz_s, rsz_x, rza_z, rzb_z, rsz_z)

    part_k[...] = dot3(aug_pair, w13_pair, NT) + dot3(split(g_ug[...]), d13_pair, NT)
    send(part_k.at[HALF:], fin_k, fin_s.at[1], fin_r_sem.at[1], sibling)
    part_v[...] = dot3(aq_pair, w2_pair, NN) + dot3(split(g_q[...]), d2_pair, NN)
    send(part_v.at[HALF:], fin_v, fin_s.at[2], fin_r_sem.at[2], sibling)
    each = u_dot * g_ug[:, :HALF] + g_dot * g_ug[:, HALF:] + q_dot * g_q[...]
    part_r[0:8, :] = jnp.broadcast_to(jnp.sum(each[:HALF].T, axis=0, keepdims=True), (8, HALF))
    part_r[8:16, :] = jnp.broadcast_to(jnp.sum(each[HALF:].T, axis=0, keepdims=True), (8, HALF))
    send(part_r.at[8:16], fin_r, fin_s.at[3], fin_r_sem.at[3], sibling)

    rows_now = sum_finish(sum_z, rza_z, rzb_z, rsz_z) + direct
    rows_z[...] = rows_now

    @pl.when(y > 0)
    def _():
        pltpu.make_async_remote_copy(
            src_ref=rows_z, dst_ref=z_in, send_sem=y_sem.at[0], recv_sem=y_sem.at[1],
            device_id=(y - 1, t), device_id_type=pl.DeviceIdType.MESH,
        ).start()

    same, rows2, other = rows_now[0:8], rows_now[8:16], rows_now[16:24]
    one_hot = (hidden_of(row_i) == col_i).astype(F32).astype(BF16)
    a = exact_select(jnp.concatenate([pick(same, other), pick(other, same)], axis=1), one_hot)
    ds_out[0, 0] = a[0:4]
    ds_out[0, 1] = half_swap(a)[0:4]
    ds_out[0, 2, :, :HALF] = rows2[0:4]
    ds_out[0, 2, :, HALF:] = half_swap(rows2)[0:4]

    wait(fin_q, fin_r_sem.at[0])
    dq_out[...] = part_q[:HALF, :] + fin_q[...]
    wait(fin_k, fin_r_sem.at[1])
    dk_out[...] = part_k[:HALF, :] + fin_k[...]
    wait(fin_v, fin_r_sem.at[2])
    dv_out[...] = part_v[:HALF, :] + fin_v[...]
    wait(fin_r, fin_r_sem.at[3])
    dr_out[...] = (part_r[0:1, :] + fin_r[0:1, :]) / r_own[0:1, :]

    for n in range(5):
        wait(pairs[n][1], sib_s.at[n])
    gather_sent(g_w, agw_s)
    sum_sent(p_g, rza_g, rzb_g, rsg_s)
    gather_sent(g_d, agd_s)
    sum_sent(p_z, rza_z, rzb_z, rsz_s)
    for n, ref in enumerate((fin_q, fin_k, fin_v, fin_r)):
        wait(ref, fin_s.at[n])

    @pl.when(y > 0)
    def _():
        wait(z_in, y_sem.at[0])


def per_device(queries, keys, values, rates, states, out_cot, final_cot):
    vmem = pl.BlockSpec(memory_space=pltpu.VMEM)
    f, b, dma = (lambda *s: pltpu.VMEM(s, F32)), (lambda *s: pltpu.VMEM(s, BF16)), (lambda *s: pltpu.SemaphoreType.DMA(s))
    scratch = [f(HALF, D)] * 4 + [f(8, HALF)] * 2
    scratch += [f(24, HALF)] * 4 + [f(16, D)]
    scratch += [f(NX, NZ, 24, HALF)] * 4 + [f(3, NZ, 24, HALF)] * 2
    scratch += [f(7, 16, HALF), f(8, 8, HALF)] * 2 + [f(NZ, 24, HALF)] * 2
    scratch += [f(D, D), f(HALF, D)] * 4
    scratch += [b(D, D)] * 6 + [b(D, D), b(D, D), b(HALF, D), b(HALF, D)] * 2
    scratch += [f(D, HALF)] * 4 + [f(D, D), f(D, HALF)] * 2
    scratch += [f(D, D)] * 3 + [f(16, HALF)] + [f(HALF, D)] * 3 + [f(8, HALF)]
    scratch += [dma(5), dma(5)] + [dma(3), dma(8), dma(8), dma()] * 2
    scratch += [dma(3), dma(8), dma(2)] * 2 + [dma(2), dma(4), dma(4)]
    d_queries, d_keys, d_values, d_rates, d_states = pl.pallas_call(
        kernel,
        out_shape=(
            jax.ShapeDtypeStruct((HALF, D), F32),
            jax.ShapeDtypeStruct((HALF, D), F32),
            jax.ShapeDtypeStruct((HALF, D), F32),
            jax.ShapeDtypeStruct((1, HALF), F32),
            jax.ShapeDtypeStruct((1, 3, 4, D), F32),
        ),
        in_specs=[vmem] * 7,
        out_specs=(vmem,) * 5,
        scratch_shapes=scratch,
        compiler_params=pltpu.CompilerParams(
            collective_id=0, has_side_effects=True, vmem_limit_bytes=40 * 1024 * 1024
        ),
        name="blocks",
    )(queries, keys, values, rates.reshape(1, HALF), states, out_cot, final_cot)
    return d_queries, d_keys, d_values, d_rates.reshape(HALF), d_states


def solution(mesh):
    return jax.shard_map(
        per_device,
        mesh=mesh,
        in_specs=(
            P(("block", "tok"), None),
            P(("block", "tok"), None),
            P(("block", "tok"), None),
            P(("block", "tok")),
            P("block", None, "tok", None),
            P(("block", "tok"), None),
            P(None, "tok", None),
        ),
        out_specs=(
            P(("block", "tok"), None),
            P(("block", "tok"), None),
            P(("block", "tok"), None),
            P(("block", "tok")),
            P("block", None, "tok", None),
        ),
        check_vma=False,
    )
```

time: 452 us -> 133 us (0.29); the launches traced: 444 us -> 133 us
  waiting for transfers between devices: 190 us -> 0 us
  Pallas kernels: 0 us -> 124 us
  blocking collectives: 115 us -> 0 us
  starting transfers between devices: 50.4 us -> 0 us
  local copies, waits for them, and re-layouts: 44.5 us -> 8.75 us
  other arithmetic: 24.1 us -> 0 us
  matrix products: 17.3 us -> 0 us
    all_to_all x6 -> x0, waiting for transfers between devices: 130 us -> none  [the longest x5 112 us: copy_for_each(): lax.all_to_all(jnp.broadcast_to(array[None], (devices, *array.shape)), ax...]
    pallas_call x0 -> x1, Pallas kernels: none -> 124 us  [per_device(): pl.pallas_call(kernel, out_shape=(jax.ShapeDtypeStruct((HALF, D), F32), j...]
    all_to_all x4 -> x0, blocking collectives: 115 us -> none  [sent_and_summed(): lax.all_to_all(tiles, axis, split_axis=0, concat_axis=0, tiled=True)]
    ppermute x3 -> x0, waiting for transfers between devices: 60.4 us -> none  [from_behind(): return lax.ppermute(array, axis, pairs)]
    all_to_all x6 -> x0, starting transfers between devices: 46.5 us -> none  [the longest x5 40.6 us: copy_for_each(): lax.all_to_all(jnp.broadcast_to(array[None], (devices, *array.shape)), ax...]
    dot_general x26 -> x0, matrix products: 17.3 us -> none  [the longest x9 7.11 us: apply_fast(): jnp.dot(inputs, weights[0], precision=HIGH, preferred_element_type=jnp.fl...]
    reshape x10 -> x0, local copies, waits for them, and re-layouts: 14.2 us -> none  [split_up(): return jnp.moveaxis(array.reshape(*before, devices, -1, *after), dim, 0)]
    add x7 -> x0, other arithmetic: 10.1 us -> none  [the longest x4 7.59 us: per_device(): summed = sent_and_summed(second_state + apply_state, 'tok', 1)]
  transfers between devices with their start and end apart: 9 -> 0, of which waited for: 9 -> 0; matrix products, arithmetic and copies ran while one was open for 2% -> 0% of each run, Pallas kernels for 0% -> 0%
where the time goes in v1:
time: 133 us
  Pallas kernels  124 us (93%)
  local copies, waits for them, and re-layouts  8.75 us (7%)
    pallas_call x1, Pallas kernels, per_device(): pl.pallas_call(kernel, out_shape=(jax.ShapeDtypeStruct((HALF, D), F32), j...  124 us
    unnamed x19, local copies, waits for them, and re-layouts  8.75 us

profile of v1, /device:TPU:1, one launch (start us, length us, event | category | flops | bytes accessed | tf_op | source)
XLA Modules:
  0.0 133.2 jit_solution(8304288907304573022)
XLA Ops:
  0.6 0.0 copy-start.6
  0.6 0.6 copy-done.6
  1.3 0.0 copy-start
  1.3 0.9 copy-done
  2.2 0.0 copy-start.1
  2.2 0.9 copy-done.1
  3.1 0.0 copy-start.2
  3.1 0.9 copy-done.2
  4.0 0.0 copy-start.3
  4.0 0.9 copy-done.3
  4.9 0.0 copy-start.4
  4.9 0.7 copy-done.4
  5.6 0.0 copy-start.5
  5.6 0.7 copy-done.5
  6.3 123.8 %blocks.1 = (f32[128,256]{1,0:T(8,128)S(1)}, f32[128,256]{1,0:T(8,128)S(1)}, f32[128,256]{1,0:T(8,128)S(1)}, f32[1,128]{1,0:T(1,128)S(1)}, f32[1,3,4,256]{3,2,1,0:T(4,128)S(1)}) custom-call(f32[128,256]{1,0:T(8,128)S(1)} %copy-done, f32[128,256]{1,0:T(8,128)S(1)} %copy-done.1, f32[128,256]{1,0:T(8,128)S(1)} %copy-done.2, f32[1,128]{1,0:T(1,128)S(1)} %bitcast.2, ...), custom_call_target="tpu_custom_call" | custom-call | tf_op jit(solution)/shard_map/blocks/pallas_call | solution.py:390
  130.1 0.7 copy.17
  130.8 0.7 copy.18
  131.4 0.7 copy.19
  132.1 0.5 copy.20
  132.6 0.6 copy.21
Async XLA Ops:
  0.6 0.7 copy-start.6
  1.3 0.9 copy-start
  2.2 0.9 copy-start.1
  3.1 0.9 copy-start.2
  4.0 0.9 copy-start.3
  4.9 0.7 copy-start.4
  5.6 0.7 copy-start.5
